TPU v7x, 32 devices: a whole 2x2x4 slice. The times are simulated.
32 devices in a mesh: dp: 8 (over z, x), ep: 4 (over y, core).
Axes of the slice: x: 2, y: 2, z: 4, core: 2. Of those that a mesh axis runs over, the one named last changes fastest.
Arguments:
- tokens: bfloat16 [64, 197, 768], P(('dp', 'ep')), may hold values from -6 to 6
- live_images: int32 [32], P(('dp', 'ep')), may hold values from 1 to 2, as said below
- routes: int32 [64, 197, 2], P(('dp', 'ep')), may hold values from 0 to 3, all different within a row; in each aligned block of 394 rows (0 to 393, 394 to 787, ..., all dimensions but the last counted through in order) at most 248 rows name the same one
- ln1_gain: float32 [768], replicated, may hold values from 0.1 to 1.9
- ln1_bias: float32 [768], replicated, may hold values from -3 to 3
- query_key_value_weight: bfloat16 [768, 2304], replicated, may hold values from -0.21875 to 0.21875
- attention_output_weight: bfloat16 [768, 768], replicated, may hold values from -0.625 to 0.625
- ln2_gain: float32 [768], replicated, may hold values from 0.1 to 1.9
- ln2_bias: float32 [768], replicated, may hold values from -3 to 3
- w_router: bfloat16 [768, 4], replicated, may hold values from -0.4375 to 0.4375
- w_in: bfloat16 [4, 768, 3072], P('ep'), may hold values from -0.21875 to 0.21875
- w_out: bfloat16 [4, 3072, 768], P('ep'), may hold values from -0.875 to 0.875
- cotangent: bfloat16 [64, 197, 768], P(('dp', 'ep')), may hold values from -6 to 6
Outputs:
- block_out: bfloat16 [64, 197, 768], P(('dp', 'ep'))
- grad_tokens: float32 [64, 197, 768], P(('dp', 'ep'))
- grad_ln1_gain: float32 [768], P('ep')
- grad_ln1_bias: float32 [768], P('ep')
- grad_w_qkv: float32 [768, 2304], P('ep')
- grad_w_attn_out: float32 [768, 768], P('ep')
- grad_ln2_gain: float32 [768], P('ep')
- grad_ln2_bias: float32 [768], P('ep')
- grad_w_router: float32 [768, 4], P('ep')
- grad_w_in: float32 [4, 768, 3072], P('ep', 'dp')
- grad_w_out: float32 [4, 3072, 768], P('ep', 'dp')
Inputs may be any that keep to these rules, and one draw needn't show every extreme that they name: Each device holds 2 image slots of which the first live_images are images; some device holds 2, some holds one. `routes`: each token names two different experts. Among the 394 tokens of one device, slots live or not, no expert is named more than 248 times, a bound that some block reaches.
All inputs are finite; a program needn't handle non-finite values.
Results may differ from a plain program's by a relative error of at most 0.024.
Values may be sent and summed in bfloat16 or wider, within the bound.
A program may use at most 192 MiB of HBM per device.

v0:
```python
import jax
import jax.numpy as jnp
from jax import lax
from jax.sharding import PartitionSpec as P

HEADS = 12
HEAD_DIM = 64
eps = 1e-06


def norm_forward(values):
    centre = jnp.mean(values, axis=-1, keepdims=True)
    shifted = values - centre
    inverse = lax.rsqrt(jnp.mean(shifted * shifted, axis=-1, keepdims=True) + eps)
    return (shifted * inverse, inverse)


def norm_backward(grad_normed, normalized_input, inverse):
    middle = jnp.mean(grad_normed, axis=-1, keepdims=True)
    along = jnp.mean(grad_normed * normalized_input, axis=-1, keepdims=True)
    return (grad_normed - middle - normalized_input * along) * inverse


def body(
    tokens,
    live_images,
    routes,
    ln1_gain,
    ln1_bias,
    query_key_value_weight,
    attention_output_weight,
    ln2_gain,
    ln2_bias,
    w_router,
    w_in,
    w_out,
    cotangent,
):
    slot_count, seq_len, model_width = tokens.shape
    row_count = slot_count * seq_len
    expert_count = w_router.shape[1]
    hidden_width = w_in.shape[2]
    capacity = ((2 * row_count + expert_count - 1) // expert_count * 5 // 4 + 7) // 8 * 8
    scaling = HEAD_DIM ** (-0.5)
    inputs = tokens.astype(jnp.float32).reshape(row_count, model_width)
    normed1, inverse1 = norm_forward(inputs)
    attn_in = (normed1 * ln1_gain + ln1_bias).astype(jnp.bfloat16)
    qkv_rows = jnp.dot(attn_in, query_key_value_weight, preferred_element_type=jnp.float32).astype(
        jnp.bfloat16
    )
    qkv_heads = qkv_rows.reshape(slot_count, seq_len, 3, HEADS, HEAD_DIM)
    queries = qkv_heads[:, :, 0]
    keys_all = qkv_heads[:, :, 1]
    values_all = qkv_heads[:, :, 2]
    scores = (
        jnp.einsum("sqhc,skhc->shqk", queries, keys_all, preferred_element_type=jnp.float32)
        * scaling
    )
    row_peak = jnp.max(scores, axis=-1, keepdims=True)
    raised = jnp.exp(scores - row_peak)
    totals = jnp.sum(raised, axis=-1, keepdims=True)
    log_total = row_peak + jnp.log(totals)
    weights = (raised / totals).astype(jnp.bfloat16)
    attended_context = jnp.einsum(
        "shqk,skhc->sqhc", weights, values_all, preferred_element_type=jnp.float32
    )
    attended_context = attended_context.astype(jnp.bfloat16).reshape(row_count, model_width)
    hidden1 = inputs + jnp.dot(
        attended_context, attention_output_weight, preferred_element_type=jnp.float32
    )
    normed2, inverse2 = norm_forward(hidden1)
    moe_in = (normed2 * ln2_gain + ln2_bias).astype(jnp.bfloat16)
    router = jax.nn.softmax(jnp.dot(moe_in, w_router, preferred_element_type=jnp.float32), axis=-1)
    chosen = routes.reshape(row_count, 2)
    expert_ids = jnp.arange(expert_count, dtype=jnp.int32)
    picked = (chosen[:, :, None] == expert_ids[None, None, :]).astype(jnp.float32)
    gates = jnp.sum(picked * router[:, None, :], axis=-1)
    token_live = (jnp.arange(row_count, dtype=jnp.int32) // seq_len < live_images[0]).astype(
        jnp.float32
    )
    pair_ids = chosen.reshape(2 * row_count)
    pair_live = jnp.repeat(token_live, 2) > 0.5
    member = ((pair_ids[:, None] == expert_ids[None, :]) & pair_live[:, None]).astype(jnp.int32)
    position = jnp.sum((jnp.cumsum(member, axis=0) - 1) * member, axis=-1)
    slot_ids = jnp.where(pair_live, pair_ids * capacity + position, -1).reshape(row_count, 2)
    lanes = jnp.arange(expert_count * capacity, dtype=jnp.int32)
    placing = (jnp.transpose(slot_ids)[:, None, :] == lanes[None, :, None]).astype(jnp.bfloat16)
    outbox = jnp.einsum("jsr,rd->sd", placing, moe_in, preferred_element_type=jnp.float32)
    outbox = outbox.astype(jnp.bfloat16).reshape(expert_count, capacity, model_width)
    inbox = lax.all_to_all(outbox, "ep", split_axis=0, concat_axis=0, tiled=True)
    flat_in = inbox.reshape(-1, model_width)
    pre_act = jnp.dot(flat_in, w_in[0], preferred_element_type=jnp.float32)
    activated = jax.nn.gelu(pre_act).astype(jnp.bfloat16)
    produced = jnp.dot(activated, w_out[0], preferred_element_type=jnp.float32).astype(jnp.bfloat16)
    coming_back = lax.all_to_all(
        produced.reshape(inbox.shape), "ep", split_axis=0, concat_axis=0, tiled=True
    )
    coming_back, pre_act = (
        coming_back,
        pre_act.reshape(inbox.shape[0], inbox.shape[1], hidden_width),
    )
    arrived_rows = inbox.reshape(-1, model_width)
    pre_rows = pre_act.reshape(-1, hidden_width)
    returned_rows = coming_back.reshape(expert_count * capacity, model_width)
    taken = jnp.einsum("jsr,sd->rjd", placing, returned_rows, preferred_element_type=jnp.float32)
    mixture = jnp.sum(gates[:, :, None] * taken, axis=1)
    block_out = (
        ((hidden1 + mixture) * token_live[:, None]).astype(jnp.bfloat16).reshape(tokens.shape)
    )
    upstream = cotangent.astype(jnp.float32).reshape(row_count, model_width) * token_live[:, None]
    gate_grads = jnp.sum(taken * upstream[:, None, :], axis=-1)
    sent_grads = (gates[:, :, None] * upstream[:, None, :]).astype(jnp.bfloat16)
    grad_outbox = jnp.einsum("jsr,rjd->sd", placing, sent_grads, preferred_element_type=jnp.float32)
    grad_outbox = grad_outbox.astype(jnp.bfloat16).reshape(expert_count, capacity, model_width)
    grad_inbox = lax.all_to_all(grad_outbox, "ep", split_axis=0, concat_axis=0, tiled=True)
    grad_rows = grad_inbox.reshape(-1, model_width)
    activated_rows, gelu_pull = jax.vjp(jax.nn.gelu, pre_rows)
    activated_low = activated_rows.astype(jnp.bfloat16)
    grad_activated = jnp.einsum(
        "rd,fd->rf", grad_rows, w_out[0], preferred_element_type=jnp.float32
    )
    grad_pre = gelu_pull(grad_activated)[0].astype(jnp.bfloat16)
    columns = activated_low
    grad_w_out = lax.psum_scatter(
        jnp.einsum("rf,rd->fd", columns, grad_rows, preferred_element_type=jnp.float32).astype(
            jnp.bfloat16
        ),
        "dp",
        scatter_dimension=0,
        tiled=True,
    ).astype(jnp.float32)
    grad_back_rows = jnp.einsum(
        "rf,df->rd", grad_pre, w_in[0], preferred_element_type=jnp.float32
    ).astype(jnp.bfloat16)
    grad_back = lax.all_to_all(
        grad_back_rows.reshape(grad_inbox.shape), "ep", split_axis=0, concat_axis=0, tiled=True
    )
    columns = arrived_rows
    grad_w_in = lax.psum_scatter(
        jnp.einsum("rd,rf->df", columns, grad_pre, preferred_element_type=jnp.float32).astype(
            jnp.bfloat16
        ),
        "dp",
        scatter_dimension=0,
        tiled=True,
    ).astype(jnp.float32)
    grad_back_flat = grad_back.reshape(expert_count * capacity, model_width)
    expert_grad = jnp.einsum(
        "jsr,sd->rd", placing, grad_back_flat, preferred_element_type=jnp.float32
    )
    grad_router_probs = jnp.sum(gate_grads[:, :, None] * picked, axis=1)
    grad_logits = router * (
        grad_router_probs - jnp.sum(router * grad_router_probs, axis=-1, keepdims=True)
    )
    grad_logits = grad_logits.astype(jnp.bfloat16)
    grad_w_router = jnp.einsum("rd,re->de", moe_in, grad_logits, preferred_element_type=jnp.float32)
    grad_moe_in = expert_grad + jnp.einsum(
        "re,de->rd", grad_logits, w_router, preferred_element_type=jnp.float32
    )
    grad_ln2_gain = jnp.sum(grad_moe_in * normed2, axis=0)
    grad_ln2_bias = jnp.sum(grad_moe_in, axis=0)
    grad_hidden1 = upstream + norm_backward(grad_moe_in * ln2_gain, normed2, inverse2)
    grad_attn = grad_hidden1.astype(jnp.bfloat16)
    grad_w_attn_out = jnp.einsum(
        "rd,re->de", attended_context, grad_attn, preferred_element_type=jnp.float32
    )
    grad_context = jnp.einsum(
        "re,de->rd", grad_attn, attention_output_weight, preferred_element_type=jnp.float32
    )
    grad_context = grad_context.astype(jnp.bfloat16).reshape(slot_count, seq_len, HEADS, HEAD_DIM)
    again = (
        jnp.einsum("sqhc,skhc->shqk", queries, keys_all, preferred_element_type=jnp.float32)
        * scaling
    )
    probs_again = jnp.exp(again - log_total)
    probs_low = probs_again.astype(jnp.bfloat16)
    grad_values = jnp.einsum(
        "shqk,sqhc->skhc", probs_low, grad_context, preferred_element_type=jnp.float32
    )
    grad_probs = jnp.einsum(
        "sqhc,skhc->shqk", grad_context, values_all, preferred_element_type=jnp.float32
    )
    grad_scores = probs_again * (
        grad_probs - jnp.sum(probs_again * grad_probs, axis=-1, keepdims=True)
    )
    grad_scores = grad_scores.astype(jnp.bfloat16)
    grad_queries = (
        jnp.einsum("shqk,skhc->sqhc", grad_scores, keys_all, preferred_element_type=jnp.float32)
        * scaling
    )
    grad_keys = (
        jnp.einsum("shqk,sqhc->skhc", grad_scores, queries, preferred_element_type=jnp.float32)
        * scaling
    )
    grad_qkv = (
        jnp.stack([grad_queries, grad_keys, grad_values], axis=2)
        .astype(jnp.bfloat16)
        .reshape(row_count, 3 * model_width)
    )
    grad_w_qkv = jnp.einsum("rd,re->de", attn_in, grad_qkv, preferred_element_type=jnp.float32)
    grad_attn_in = jnp.einsum(
        "re,de->rd", grad_qkv, query_key_value_weight, preferred_element_type=jnp.float32
    )
    grad_ln1_gain = jnp.sum(grad_attn_in * normed1, axis=0)
    grad_ln1_bias = jnp.sum(grad_attn_in, axis=0)
    grad_inputs = grad_hidden1 + norm_backward(grad_attn_in * ln1_gain, normed1, inverse1)
    shared = (
        grad_w_qkv,
        grad_w_attn_out,
        grad_w_router,
        grad_ln1_gain,
        grad_ln1_bias,
        grad_ln2_gain,
        grad_ln2_bias,
    )
    partial_sums = (
        lax.psum_scatter(
            shared[0].astype(jnp.bfloat16), "ep", scatter_dimension=0, tiled=True
        ).astype(jnp.float32),
        lax.psum_scatter(
            shared[1].astype(jnp.bfloat16), "ep", scatter_dimension=0, tiled=True
        ).astype(jnp.float32),
        lax.psum_scatter(
            shared[2].astype(jnp.bfloat16), "ep", scatter_dimension=0, tiled=True
        ).astype(jnp.float32),
        lax.psum_scatter(
            shared[3].astype(jnp.bfloat16), "ep", scatter_dimension=0, tiled=True
        ).astype(jnp.float32),
        lax.psum_scatter(
            shared[4].astype(jnp.bfloat16), "ep", scatter_dimension=0, tiled=True
        ).astype(jnp.float32),
        lax.psum_scatter(
            shared[5].astype(jnp.bfloat16), "ep", scatter_dimension=0, tiled=True
        ).astype(jnp.float32),
        lax.psum_scatter(
            shared[6].astype(jnp.bfloat16), "ep", scatter_dimension=0, tiled=True
        ).astype(jnp.float32),
    )
    shares = (
        lax.psum(partial_sums[0].astype(jnp.bfloat16), "dp").astype(jnp.float32),
        lax.psum(partial_sums[1].astype(jnp.bfloat16), "dp").astype(jnp.float32),
        lax.psum(partial_sums[2].astype(jnp.bfloat16), "dp").astype(jnp.float32),
        lax.psum(partial_sums[3].astype(jnp.bfloat16), "dp").astype(jnp.float32),
        lax.psum(partial_sums[4].astype(jnp.bfloat16), "dp").astype(jnp.float32),
        lax.psum(partial_sums[5].astype(jnp.bfloat16), "dp").astype(jnp.float32),
        lax.psum(partial_sums[6].astype(jnp.bfloat16), "dp").astype(jnp.float32),
    )
    return (
        block_out,
        grad_inputs.reshape(tokens.shape),
        shares[3],
        shares[4],
        shares[0],
        shares[1],
        shares[5],
        shares[6],
        shares[2],
        grad_w_in[None],
        grad_w_out[None],
    )


def solution(mesh):
    in_specs = (
        P(("dp", "ep"), None, None),
        P(("dp", "ep")),
        P(("dp", "ep"), None, None),
        P(),
        P(),
        P(),
        P(),
        P(),
        P(),
        P(),
        P("ep", None, None),
        P("ep", None, None),
        P(("dp", "ep"), None, None),
    )
    out_specs = (
        P(("dp", "ep"), None, None),
        P(("dp", "ep"), None, None),
        P("ep"),
        P("ep"),
        P("ep", None),
        P("ep", None),
        P("ep"),
        P("ep"),
        P("ep", None),
        P("ep", "dp", None),
        P("ep", "dp", None),
    )
    return jax.shard_map(body, mesh=mesh, in_specs=in_specs, out_specs=out_specs, check_vma=False)
```

profile of v0, /device:TPU:0, one launch (start us, length us, event | category | flops | bytes accessed | tf_op | source)
XLA Modules:
  0.0 590.4 jit_solution(2008736721865741235)
XLA Ops:
  40.4 4.2 convolution_convert_fusion.3
  44.6 6.6 %reshape.268 = bf16[2,197,3,12,64]{4,3,2,1,0:T(8,128)(2,1)} reshape(bf16[394,2304]{1,0:T(8,128)(2,1)} %convolution_convert_fusion.3) | data formatting | bytes 3631104 | tf_op jit(solution)/shard_map/reshape | solution.py:51
  51.3 5.0 fusion.71
  83.4 4.4 all-to-all-start
  97.5 3.7 bitcast_convert_fusion
  101.2 6.8 %all-to-all-done = bf16[4,248,768]{2,1,0:T(8,128)(2,1)} async-done(((bf16[4,248,768]{2,1,0:T(8,128)(2,1)}), bf16[4,248,768]{2,1,0:T(8,128)(2,1)}, u32[]{:S(2)}, u32[]{:S(2)}) %all-to-all-start) | async-done | bytes 1523744 | tf_op jit(solution)/shard_map/all_to_all | solution.py:90
  108.0 4.4 all-to-all-start.2
  112.4 7.2 %fusion.13 = f32[992,3072]{1,0:T(8,128)S(1)} fusion(bf16[992,768]{1,0:T(8,128)(2,1)} %bitcast.8, bf16[1,768,3072]{2,1,0:T(8,128)(2,1)} %param.23), kind=kOutput, calls=%fused_computation.25 | convolution fusion | flops 4680843264 | bytes 18432000 | tf_op jit(solution)/shard_map/dot_general | solution.py:92
  119.6 4.4 copy-done.56
  124.0 10.6 %fusion.32 = bf16[992,768]{1,0:T(8,128)(2,1)} fusion(bf16[1,3072,768]{2,1,0:T(8,128)(2,1)} %param.24, f32[992,3072]{1,0:T(8,128)S(1)} %fusion.13), kind=kOutput, calls=%fused_computation.48 | convolution fusion | flops 4709031936 | bytes 18432000 | tf_op jit(solution)/shard_map/dot_general | solution.py:94
  134.5 4.6 all-to-all-start.1
  139.1 14.9 %fusion.6 = bf16[992,3072]{1,0:T(8,128)(2,1)S(1)} fusion(f32[992,3072]{1,0:T(8,128)} %copy-done.56, bf16[992,768]{1,0:T(8,128)(2,1)} %bitcast.17, bf16[1,3072,768]{2,1,0:T(8,128)(2,1)} %param.24), kind=kOutput, calls=%fused_computation.8 | convolution fusion | flops 4741791744 | bytes 24526848 | tf_op jit(solution)/shard_map/rd,fd->rf/dot_general | solution.py:119
  156.6 8.3 %fusion.29 = bf16[992,768]{1,0:T(8,128)(2,1)} fusion(bf16[992,3072]{1,0:T(8,128)(2,1)S(1)} %fusion.6, bf16[1,768,3072]{2,1,0:T(8,128)(2,1)} %param.23), kind=kOutput, calls=%fused_computation.47 | convolution fusion | flops 4681605120 | bytes 12337152 | tf_op jit(solution)/shard_map/rf,df->rd/dot_general | solution.py:132
  165.0 4.5 all-to-all-start.3
  176.0 4.7 fusion.25
  181.4 7.6 %all-to-all-done.3 = bf16[4,248,768]{2,1,0:T(8,128)(2,1)} async-done(((bf16[4,248,768]{2,1,0:T(8,128)(2,1)}), bf16[4,248,768]{2,1,0:T(8,128)(2,1)}, u32[]{:S(2)}, u32[]{:S(2)}) %all-to-all-start.3) | async-done | bytes 1523744 | tf_op jit(solution)/shard_map/all_to_all | solution.py:135
  200.8 3.5 reshape.269
  207.3 4.7 multiply_reduce_fusion
  212.0 3.6 multiply_convert_fusion.1
  219.5 3.9 copy.137
  223.3 6.7 %convert_element_type.186 = bf16[394,2304]{0,1:T(8,128)(2,1)} reshape(bf16[2,197,3,12,64]{1,0,4,3,2:T(2,128)(2,1)} %copy.137) | data formatting | bytes 3631104 | tf_op jit(solution)/shard_map/convert_element_type | solution.py:197
  230.0 5.8 convolution_convert_fusion.2
  239.4 38.2 %reduce-scatter.8.cloned.1.call-done = bf16[192,2304]{1,0:T(8,128)(2,1)} async-done(((bf16[768,2304]{1,0:T(8,128)(2,1)}), bf16[192,2304]{1,0:T(8,128)(2,1)}) %reduce-scatter.8.cloned.1.call-update) | async-done | bytes 884752 | tf_op jit(solution)/shard_map/reduce_scatter | solution.py:217
  277.6 11.8 %convolution_convert_fusion = bf16[3072,768]{1,0:T(8,128)(2,1)} fusion(bf16[992,768]{1,0:T(8,128)(2,1)} %bitcast.17, f32[992,3072]{1,0:T(8,128)} %copy-done.56), kind=kOutput, calls=%fused_computation.10 | convolution fusion | flops 4710629376 | bytes 18432000 | tf_op jit(solution)/shard_map/rf,rd->fd/dot_general | solution.py:125
  289.5 9.1 %convolution_convert_fusion.1 = bf16[768,3072]{1,0:T(8,128)(2,1)} fusion(bf16[992,768]{1,0:T(8,128)(2,1)} %bitcast.8, bf16[992,3072]{1,0:T(8,128)(2,1)} %copy-done.55), kind=kOutput, calls=%fused_computation.11 | convolution fusion | flops 4683202560 | bytes 12337152 | tf_op jit(solution)/shard_map/rd,rf->df/dot_general | solution.py:140
  304.9 5.9 multiply_reduce_fusion.3
  310.8 6.8 %all-reduce.7 = (bf16[768]{0:T(1024)(128)(2,1)}, bf16[768]{0:T(1024)(128)(2,1)}, bf16[768]{0:T(1024)(128)(2,1)}, bf16[768]{0:T(1024)(128)(2,1)}) all-reduce(bf16[768]{0:T(1024)(128)(2,1)} %get-tuple-element.68, bf16[768]{0:T(1024)(128)(2,1)} %get-tuple-element.75, ...), channel_id=2, replica_groups=mesh['dp'=8,'ep'=4] {'ep'}, use_global_device_ids=true, to_apply=%region_23.24.clone | all-reduce | flops 3072 | bytes 12288
  323.5 3.5 multiply_add_fusion
  333.4 22.1 %all-reduce.5 = (bf16[192]{0:T(256)(128)(2,1)}, bf16[192]{0:T(256)(128)(2,1)}, bf16[192]{0:T(256)(128)(2,1)}, bf16[192]{0:T(256)(128)(2,1)}, bf16[192,4]{0,1:T(4,128)(2,1)S(1)}) all-reduce(bf16[192]{0:T(256)(128)(2,1)S(1)} %dynamic-slice.1, bf16[192]{0:T(256)(128)(2,1)S(1)} %copy-done.53, ...), channel_id=1, replica_groups=mesh['dp'=8,'ep'=4] {'dp'}, use_global_device_ids=true, to_apply=%region_24.25 | all-reduce | flops 1536 | bytes 6144 | tf_op jit(solution)/shard_map/psum | solution.py:243
  360.9 23.1 %all-reduce.10.cloned.1.call-done = (bf16[192,2304]{1,0:T(8,128)(2,1)}, bf16[192,768]{1,0:T(8,128)(2,1)}) async-done(((bf16[192,2304]{1,0:T(8,128)(2,1)}, bf16[192,768]{1,0:T(8,128)(2,1)}), (bf16[192,2304]{1,0:T(8,128)(2,1)}, bf16[192,768]{1,0:T(8,128)(2,1)})) %all-reduce.10.cloned.1.call-update) | async-done | bytes 1179664 | tf_op jit(solution)/shard_map/psum | solution.py:240
  388.4 94.0 %reduce-scatter.14.cloned.1.call-done = bf16[384,768]{1,0:T(8,128)(2,1)} async-done(((bf16[3072,768]{1,0:T(8,128)(2,1)}), bf16[384,768]{1,0:T(8,128)(2,1)}) %reduce-scatter.14.cloned.1.call-update) | async-done | bytes 589840 | tf_op jit(solution)/shard_map/reduce_scatter | solution.py:124
  484.5 96.7 %reduce-scatter.12.cloned.1.call-done = bf16[96,3072]{1,0:T(8,128)(2,1)} async-done(((bf16[768,3072]{1,0:T(8,128)(2,1)}), bf16[96,3072]{1,0:T(8,128)(2,1)}) %reduce-scatter.12.cloned.1.call-update) | async-done | bytes 589840 | tf_op jit(solution)/shard_map/reduce_scatter | solution.py:139
  (226 shorter events, 132.9 us)
Async XLA Ops:
  7.2 33.2 %copy-start = (bf16[768,2304]{1,0:T(8,128)(2,1)S(1)}, bf16[768,2304]{1,0:T(8,128)(2,1)}, u32[]{:S(2)}) copy-start(bf16[768,2304]{1,0:T(8,128)(2,1)} %param.18) | copy-start | bytes 10616836
  20.9 5.0 copy-start.42
  32.7 7.6 %copy-start.39 = (f32[768]{0:T(1024)S(1)}, f32[768]{0:T(1024)}, u32[]{:S(2)}) copy-start(f32[768]{0:T(1024)} %param.16) | copy-start | bytes 9220
  32.7 7.6 %copy-start.43 = (f32[394]{0:T(512)S(1)}, f32[394]{0:T(512)}, u32[]{:S(2)}) copy-start(f32[394]{0:T(512)} %div.53) | copy-start | bytes 4732
  32.8 7.6 %copy-start.45 = (f32[394]{0:T(512)S(1)}, f32[394]{0:T(512)}, u32[]{:S(2)}) copy-start(f32[394]{0:T(512)} %rsqrt.21) | copy-start | bytes 4732
  83.4 24.6 %all-to-all-start = ((bf16[4,248,768]{2,1,0:T(8,128)(2,1)}), bf16[4,248,768]{2,1,0:T(8,128)(2,1)}, u32[]{:S(2)}, u32[]{:S(2)}) async-start(bf16[4,248,768]{2,1,0:T(8,128)(2,1)} %bitcast.131), calls=%async_computation | async-start | bytes 3047424 | tf_op jit(solution)/shard_map/all_to_all | solution.py:90
  87.8 7.2 %copy-start.21 = (s32[394,2]{0,1:T(2,128)S(1)}, s32[394,2]{0,1:T(2,128)}, u32[]{:S(2)}) copy-start(s32[394,2]{0,1:T(2,128)} %eq.50) | copy-start | bytes 9460
  89.2 7.3 %copy-start.18 = (f32[394]{0:T(512)}, f32[394]{0:T(512)S(1)}, u32[]{:S(2)}) copy-start(f32[394]{0:T(512)S(1)} %get-tuple-element.96) | copy-start | bytes 4732
  108.0 26.5 %all-to-all-start.2 = ((bf16[4,248,768]{2,1,0:T(8,128)(2,1)}), bf16[4,248,768]{2,1,0:T(8,128)(2,1)}, u32[]{:S(2)}, u32[]{:S(2)}) async-start(bf16[4,248,768]{2,1,0:T(8,128)(2,1)} %bitcast.132), calls=%async_computation.2 | async-start | bytes 3047424 | tf_op jit(solution)/shard_map/all_to_all | solution.py:115
  119.6 4.4 copy-start.56
  134.5 30.4 %all-to-all-start.1 = ((bf16[4,248,768]{2,1,0:T(8,128)(2,1)}), bf16[4,248,768]{2,1,0:T(8,128)(2,1)}, u32[]{:S(2)}, u32[]{:S(2)}) async-start(bf16[4,248,768]{2,1,0:T(8,128)(2,1)} %bitcast.133), calls=%async_computation.1 | async-start | bytes 3047424 | tf_op jit(solution)/shard_map/all_to_all | solution.py:95
  165.0 4.5 copy-start.40
  165.0 24.1 %all-to-all-start.3 = ((bf16[4,248,768]{2,1,0:T(8,128)(2,1)}), bf16[4,248,768]{2,1,0:T(8,128)(2,1)}, u32[]{:S(2)}, u32[]{:S(2)}) async-start(bf16[4,248,768]{2,1,0:T(8,128)(2,1)} %bitcast.130), calls=%async_computation.3 | async-start | bytes 3047424 | tf_op jit(solution)/shard_map/all_to_all | solution.py:135
  169.4 6.6 %copy-start.38 = (s32[2,394]{1,0:T(2,128)S(1)}, s32[2,394]{1,0:T(2,128)}, u32[]{:S(2)}) copy-start(s32[2,394]{1,0:T(2,128)} %copy-done.36) | copy-start | bytes 9460
  169.5 69.9 %reduce-scatter.10.cloned.1.call-start = ((), (), s32[]{:S(2)}) async-start(), calls=%async_computation.10 | async-start | bytes 1474560 | tf_op jit(solution)/shard_map/reduce_scatter | solution.py:220
  171.7 4.3 copy-start.51
  176.0 4.7 copy-start.22
  176.0 4.7 copy-start.19
  176.0 4.7 copy-start.26
  200.8 76.8 %reduce-scatter.8.cloned.1.call-start = ((), (), s32[]{:S(2)}) async-start(), calls=%async_computation.9 | async-start | bytes 4423680 | tf_op jit(solution)/shard_map/reduce_scatter | solution.py:217
  207.3 4.7 copy-start.15
  207.3 10.1 %slice-start = ((s8[4915200]{0:T(1024)(128)(4,1)}), s8[4194304]{0:T(1024)(128)(4,1)S(1)}, s32[]{:S(2)}) async-start(s8[4915200]{0:T(1024)(128)(4,1)} %bitcast.128), calls=%async_computation.15 | async-start | bytes 8388608
  212.0 5.3 slice-start.1
  235.8 96.7 %reduce-scatter.16.cloned.1.call-start = ((), (), s32[]{:S(2)}) async-start(), calls=%async_computation.13 | async-start | bytes 245760
  239.3 144.8 %all-reduce.10.cloned.1.call-start = ((), (), s32[]{:S(2)}) async-start(), calls=%async_computation.14 | async-start | bytes 2359296 | tf_op jit(solution)/shard_map/psum | solution.py:240
  277.6 204.8 %reduce-scatter.14.cloned.1.call-start = ((), (), s32[]{:S(2)}) async-start(), calls=%async_computation.12 | async-start | bytes 5308416 | tf_op jit(solution)/shard_map/reduce_scatter | solution.py:124
  289.4 291.8 %reduce-scatter.12.cloned.1.call-start = ((), (), s32[]{:S(2)}) async-start(), calls=%async_computation.11 | async-start | bytes 5308416 | tf_op jit(solution)/shard_map/reduce_scatter | solution.py:139
  298.6 6.2 %copy-start.41 = (f32[768]{0:T(1024)S(1)}, f32[768]{0:T(1024)}, u32[]{:S(2)}) copy-start(f32[768]{0:T(1024)} %param.16) | copy-start | bytes 9220
  298.6 6.2 %copy-start.44 = (f32[394]{0:T(512)S(1)}, f32[394]{0:T(512)}, u32[]{:S(2)}) copy-start(f32[394]{0:T(512)} %div.53) | copy-start | bytes 4732
  298.7 6.2 %copy-start.46 = (f32[394]{0:T(512)S(1)}, f32[394]{0:T(512)}, u32[]{:S(2)}) copy-start(f32[394]{0:T(512)} %rsqrt.21) | copy-start | bytes 4732
  304.9 5.9 copy-start.47
  326.9 6.4 %copy-start.53 = (bf16[192]{0:T(256)(128)(2,1)S(1)}, bf16[192]{0:T(256)(128)(2,1)}, u32[]{:S(2)}) copy-start(bf16[192]{0:T(256)(128)(2,1)} %dynamic-slice.3) | copy-start | bytes 1156
  (37 other events, 72.9 us)
Sparse Core Ops, SparseCore 0:
  200.9 26.7 reduce-scatter.9
  235.9 41.5 reduce-scatter.7
  280.6 19.7 reduce-scatter.15
  303.8 80.2 all-reduce.9
  387.6 94.7 reduce-scatter.13
  485.9 95.3 reduce-scatter.11
where the time goes:
time: 596 us; the launch traced here: 590 us
  waiting for transfers between devices  267 us (45%)
  matrix products  114 us (19%)
  local copies, waits for them, and re-layouts  100 us (17%)
  other arithmetic  46.6 us (8%)
  blocking collectives  28.9 us (5%)
  starting transfers between devices  18 us (3%)
  between operations  16.4 us (3%)
    reduce_scatter x1, waiting for transfers between devices, body(): lax.psum_scatter(jnp.einsum('rd,rf->df', columns, grad_pre, preferred_ele...  96.7 us
    reduce_scatter x1, waiting for transfers between devices, body(): lax.psum_scatter(jnp.einsum('rf,rd->fd', columns, grad_rows, preferred_el...  94 us
    unnamed x135, local copies, waits for them, and re-layouts  41.7 us
    reduce_scatter x1, waiting for transfers between devices, body(): lax.psum_scatter(shared[0].astype(jnp.bfloat16), 'ep', scatter_dimension=...  38.2 us
    psum x1, waiting for transfers between devices, body(): lax.psum(partial_sums[0].astype(jnp.bfloat16), 'dp').astype(jnp.float32)  23.1 us
    psum x1, blocking collectives, body(): lax.psum(partial_sums[3].astype(jnp.bfloat16), 'dp').astype(jnp.float32)  22.1 us
    dot_general x1, matrix products, body(): jnp.einsum('rd,fd->rf', grad_rows, w_out[0], preferred_element_type=jnp.f...  14.9 us
  transfers between devices with their start and end apart: 10, of which 6 were waited for; matrix products, arithmetic and copies ran while one was open for 27% of the time, Pallas kernels for 0%

commit v1 on v0

--- a/solution.py
+++ b/solution.py
@@ -132,9 +132,19 @@
     grad_back_rows = jnp.einsum(
         "rf,df->rd", grad_pre, w_in[0], preferred_element_type=jnp.float32
     ).astype(jnp.bfloat16)
-    grad_back = lax.all_to_all(
-        grad_back_rows.reshape(grad_inbox.shape), "ep", split_axis=0, concat_axis=0, tiled=True
-    )
+    x = grad_back_rows.reshape(grad_inbox.shape)
+    ways, here = (lax.axis_size("ep"), lax.axis_index("ep"))
+    width = x.shape[0] // ways
+    lengths = list(x.shape)
+    lengths[0] = width
+    height = lengths[0]
+    lengths[0] = height * ways
+    grad_back = jnp.zeros(lengths, x.dtype)
+    for mask in range(ways):
+        part = lax.dynamic_slice_in_dim(x, (here ^ mask) * width, width, axis=0)
+        if mask:
+            part = lax.ppermute(part, "ep", [(d, d ^ mask) for d in range(ways)])
+        grad_back = lax.dynamic_update_slice_in_dim(grad_back, part, (here ^ mask) * height, axis=0)
     columns = arrived_rows
     grad_w_in = lax.psum_scatter(
         jnp.einsum("rd,rf->df", columns, grad_pre, preferred_element_type=jnp.float32).astype(

time: 596 us -> 597 us (level)
  waiting for transfers between devices: 267 us -> 273 us
    ppermute x0 -> x3, waiting for transfers between devices: none -> 13.5 us  [body(): part = lax.ppermute(part, 'ep', [(d, d ^ mask) for d in range(ways)])]
    all_to_all x1 -> x0, waiting for transfers between devices: 7.64 us -> none  [body(): lax.all_to_all(grad_back_rows.reshape(grad_inbox.shape), 'ep', split_axis...]
    unnamed x135 -> x141, local copies, waits for them, and re-layouts: 41.7 us -> 37.8 us
  transfers between devices with their start and end apart: 10 -> 12, of which waited for: 6 -> 7; matrix products, arithmetic and copies ran while one was open for 27% -> 23% of each run, Pallas kernels for 0% -> 0%
where the time goes in v1:
time: 597 us; the launch traced here: 591 us
  waiting for transfers between devices  273 us (46%)
  matrix products  111 us (19%)
  local copies, waits for them, and re-layouts  100 us (17%)
  other arithmetic  43.9 us (7%)
  blocking collectives  28.9 us (5%)
  between operations  16.7 us (3%)
  starting transfers between devices  16.4 us (3%)
    reduce_scatter x1, waiting for transfers between devices, body(): lax.psum_scatter(jnp.einsum('rf,rd->fd', columns, grad_rows, preferred_el...  96.7 us
    reduce_scatter x1, waiting for transfers between devices, body(): lax.psum_scatter(jnp.einsum('rd,rf->df', columns, grad_pre, preferred_ele...  94.9 us
    reduce_scatter x1, waiting for transfers between devices, body(): lax.psum_scatter(shared[0].astype(jnp.bfloat16), 'ep', scatter_dimension=...  38.2 us
    unnamed x141, local copies, waits for them, and re-layouts  37.8 us
    psum x1, waiting for transfers between devices, body(): lax.psum(partial_sums[0].astype(jnp.bfloat16), 'dp').astype(jnp.float32)  23.1 us
    psum x1, blocking collectives, body(): lax.psum(partial_sums[3].astype(jnp.bfloat16), 'dp').astype(jnp.float32)  22.3 us
    dot_general x1, matrix products, body(): jnp.einsum('rd,fd->rf', grad_rows, w_out[0], preferred_element_type=jnp.f...  16.6 us
    ppermute x3, waiting for transfers between devices, body(): part = lax.ppermute(part, 'ep', [(d, d ^ mask) for d in range(ways)])  13.5 us
  transfers between devices with their start and end apart: 12, of which 7 were waited for; matrix products, arithmetic and copies ran while one was open for 23% of the time, Pallas kernels for 0%

profile of v1, /device:TPU:0, one launch (start us, length us, event | category | flops | bytes accessed | tf_op | source)
XLA Modules:
  0.0 590.8 jit_solution(8219124613068314517)
XLA Ops:
  22.2 4.3 convolution_convert_fusion.3
  26.5 6.8 %reshape.268 = bf16[2,197,3,12,64]{4,3,2,1,0:T(8,128)(2,1)} reshape(bf16[394,2304]{1,0:T(8,128)(2,1)} %convolution_convert_fusion.3) | data formatting | bytes 3631104 | tf_op jit(solution)/shard_map/reshape | solution.py:51
  33.3 5.0 fusion.71
  54.5 3.2 reshape.239
  81.7 4.8 all-to-all-start
  96.2 3.7 bitcast_convert_fusion
  99.9 6.8 %all-to-all-done = bf16[4,248,768]{2,1,0:T(8,128)(2,1)} async-done(((bf16[4,248,768]{2,1,0:T(8,128)(2,1)}), bf16[4,248,768]{2,1,0:T(8,128)(2,1)}, u32[]{:S(2)}, u32[]{:S(2)}) %all-to-all-start) | async-done | bytes 1523744 | tf_op jit(solution)/shard_map/all_to_all | solution.py:90
  106.7 4.3 all-to-all-start.2
  111.1 7.2 %fusion.13 = f32[992,3072]{1,0:T(8,128)S(1)} fusion(bf16[992,768]{1,0:T(8,128)(2,1)} %bitcast.8, bf16[1,768,3072]{2,1,0:T(8,128)(2,1)} %param.23), kind=kOutput, calls=%fused_computation.25 | convolution fusion | flops 4680843264 | bytes 18432000 | tf_op jit(solution)/shard_map/dot_general | solution.py:92
  118.3 4.5 copy-done.59
  122.8 10.5 %fusion.32 = bf16[992,768]{1,0:T(8,128)(2,1)} fusion(bf16[1,3072,768]{2,1,0:T(8,128)(2,1)} %param.24, f32[992,3072]{1,0:T(8,128)S(1)} %fusion.13), kind=kOutput, calls=%fused_computation.48 | convolution fusion | flops 4709031936 | bytes 18432000 | tf_op jit(solution)/shard_map/dot_general | solution.py:94
  133.3 16.6 %fusion.6 = bf16[992,3072]{1,0:T(8,128)(2,1)} fusion(f32[992,3072]{1,0:T(8,128)} %copy-done.59, bf16[992,768]{1,0:T(8,128)(2,1)} %bitcast.17, bf16[1,3072,768]{2,1,0:T(8,128)(2,1)} %param.24), kind=kOutput, calls=%fused_computation.8 | convolution fusion | flops 4741791744 | bytes 24526848 | tf_op jit(solution)/shard_map/rd,fd->rf/dot_general | solution.py:119
  149.8 4.3 all-to-all-start.1
  154.4 9.0 %fusion.29 = bf16[992,768]{1,0:T(8,128)(2,1)S(1)} fusion(bf16[992,3072]{1,0:T(8,128)(2,1)} %fusion.6, bf16[1,768,3072]{2,1,0:T(8,128)(2,1)} %param.23), kind=kOutput, calls=%fused_computation.47 | convolution fusion | flops 4681605120 | bytes 12337152 | tf_op jit(solution)/shard_map/rf,df->rd/dot_general | solution.py:132
  174.2 8.3 %collective-permute-done.1 = bf16[1,248,768]{2,1,0:T(8,128)(2,1)} collective-permute-done((bf16[1,248,768]{2,1,0:T(8,128)(2,1)}, bf16[1,248,768]{2,1,0:T(8,128)(2,1)}, u32[]{:S(2)}, u32[]{:S(2)}) %collective-permute-start.1) | collective-permute-done | bytes 380960 | tf_op jit(solution)/shard_map/ppermute | solution.py:146
  184.3 5.1 collective-permute-done.2
  190.3 3.9 fusion.25
  207.5 4.4 multiply_reduce_fusion
  212.0 3.8 multiply_convert_fusion.1
  219.6 3.9 copy.137
  223.5 6.5 %convert_element_type.186 = bf16[394,2304]{0,1:T(8,128)(2,1)} reshape(bf16[2,197,3,12,64]{1,0,4,3,2:T(2,128)(2,1)} %copy.137) | data formatting | bytes 3631104 | tf_op jit(solution)/shard_map/convert_element_type | solution.py:207
  230.1 5.8 convolution_convert_fusion.2
  239.4 38.2 %reduce-scatter.8.cloned.1.call-done = bf16[192,2304]{1,0:T(8,128)(2,1)} async-done(((bf16[768,2304]{1,0:T(8,128)(2,1)}), bf16[192,2304]{1,0:T(8,128)(2,1)}) %reduce-scatter.8.cloned.1.call-update) | async-done | bytes 884752 | tf_op jit(solution)/shard_map/reduce_scatter | solution.py:227
  277.9 9.1 %convolution_convert_fusion.1 = bf16[768,3072]{1,0:T(8,128)(2,1)} fusion(bf16[992,768]{1,0:T(8,128)(2,1)} %bitcast.8, bf16[992,3072]{1,0:T(8,128)(2,1)} %fusion.6), kind=kOutput, calls=%fused_computation.11 | convolution fusion | flops 4683202560 | bytes 12337152 | tf_op jit(solution)/shard_map/rd,rf->df/dot_general | solution.py:150
  287.1 11.8 %convolution_convert_fusion = bf16[3072,768]{1,0:T(8,128)(2,1)} fusion(bf16[992,768]{1,0:T(8,128)(2,1)} %bitcast.17, f32[992,3072]{1,0:T(8,128)} %copy-done.59), kind=kOutput, calls=%fused_computation.10 | convolution fusion | flops 4710629376 | bytes 18432000 | tf_op jit(solution)/shard_map/rf,rd->fd/dot_general | solution.py:125
  300.8 5.9 multiply_reduce_fusion.3
  306.7 6.5 %all-reduce.7 = (bf16[768]{0:T(1024)(128)(2,1)}, bf16[768]{0:T(1024)(128)(2,1)}, bf16[768]{0:T(1024)(128)(2,1)}, bf16[768]{0:T(1024)(128)(2,1)}) all-reduce(bf16[768]{0:T(1024)(128)(2,1)} %get-tuple-element.68, bf16[768]{0:T(1024)(128)(2,1)} %get-tuple-element.75, ...), channel_id=2, replica_groups=mesh['dp'=8,'ep'=4] {'ep'}, use_global_device_ids=true, to_apply=%region_23.24.clone | all-reduce | flops 3072 | bytes 12288
  319.0 3.5 multiply_add_fusion
  333.2 22.3 %all-reduce.5 = (bf16[192]{0:T(256)(128)(2,1)}, bf16[192]{0:T(256)(128)(2,1)}, bf16[192]{0:T(256)(128)(2,1)}, bf16[192]{0:T(256)(128)(2,1)}, bf16[192,4]{0,1:T(4,128)(2,1)S(1)}) all-reduce(bf16[192]{0:T(256)(128)(2,1)S(1)} %copy-done.56, bf16[192]{0:T(256)(128)(2,1)S(1)} %copy-done.57, ...), channel_id=1, replica_groups=mesh['dp'=8,'ep'=4] {'dp'}, use_global_device_ids=true, to_apply=%region_24.25 | all-reduce | flops 1536 | bytes 6144 | tf_op jit(solution)/shard_map/psum | solution.py:253
  361.0 23.1 %all-reduce.10.cloned.1.call-done = (bf16[192,2304]{1,0:T(8,128)(2,1)}, bf16[192,768]{1,0:T(8,128)(2,1)}) async-done(((bf16[192,2304]{1,0:T(8,128)(2,1)}, bf16[192,768]{1,0:T(8,128)(2,1)}), (bf16[192,2304]{1,0:T(8,128)(2,1)}, bf16[192,768]{1,0:T(8,128)(2,1)})) %all-reduce.10.cloned.1.call-update) | async-done | bytes 1179664 | tf_op jit(solution)/shard_map/psum | solution.py:250
  387.6 94.9 %reduce-scatter.12.cloned.1.call-done = bf16[96,3072]{1,0:T(8,128)(2,1)} async-done(((bf16[768,3072]{1,0:T(8,128)(2,1)}), bf16[96,3072]{1,0:T(8,128)(2,1)}) %reduce-scatter.12.cloned.1.call-update) | async-done | bytes 589840 | tf_op jit(solution)/shard_map/reduce_scatter | solution.py:149
  484.7 96.7 %reduce-scatter.14.cloned.1.call-done = bf16[384,768]{1,0:T(8,128)(2,1)} async-done(((bf16[3072,768]{1,0:T(8,128)(2,1)}), bf16[384,768]{1,0:T(8,128)(2,1)}) %reduce-scatter.14.cloned.1.call-update) | async-done | bytes 589840 | tf_op jit(solution)/shard_map/reduce_scatter | solution.py:124
  (241 shorter events, 129.3 us)
Async XLA Ops:
  7.2 15.0 %copy-start = (bf16[768,2304]{1,0:T(8,128)(2,1)S(1)}, bf16[768,2304]{1,0:T(8,128)(2,1)}, u32[]{:S(2)}) copy-start(bf16[768,2304]{1,0:T(8,128)(2,1)} %param.18) | copy-start | bytes 10616836
  9.0 6.7 %copy-start.42 = (s32[2,197,2]{1,2,0:T(2,128)S(1)}, s32[2,197,2]{1,2,0:T(2,128)}, u32[]{:S(2)}) copy-start(s32[2,197,2]{1,2,0:T(2,128)} %param.15) | copy-start | bytes 9460
  15.6 6.6 %copy-start.44 = (f32[768]{0:T(1024)S(1)}, f32[768]{0:T(1024)}, u32[]{:S(2)}) copy-start(f32[768]{0:T(1024)} %param.16) | copy-start | bytes 9220
  19.7 6.8 %copy-start.48 = (f32[394]{0:T(512)}, f32[394]{0:T(512)S(1)}, u32[]{:S(2)}) copy-start(f32[394]{0:T(512)S(1)} %rsqrt.21) | copy-start | bytes 4732
  19.8 6.7 %copy-start.50 = (f32[394]{0:T(512)}, f32[394]{0:T(512)S(1)}, u32[]{:S(2)}) copy-start(f32[394]{0:T(512)S(1)} %div.53) | copy-start | bytes 4732
  76.0 17.1 %copy-start.28 = (s32[394,2]{0,1:T(2,128)}, s32[394,2]{0,1:T(2,128)S(1)}, u32[]{:S(2)}) copy-start(s32[394,2]{0,1:T(2,128)S(1)} %eq.50) | copy-start | bytes 9460
  81.7 25.0 %all-to-all-start = ((bf16[4,248,768]{2,1,0:T(8,128)(2,1)}), bf16[4,248,768]{2,1,0:T(8,128)(2,1)}, u32[]{:S(2)}, u32[]{:S(2)}) async-start(bf16[4,248,768]{2,1,0:T(8,128)(2,1)} %bitcast.131), calls=%async_computation | async-start | bytes 3047424 | tf_op jit(solution)/shard_map/all_to_all | solution.py:90
  87.8 5.3 copy-start.26
  93.7 6.2 %copy-start.53 = (f32[394,2]{0,1:T(2,128)}, f32[394,2]{0,1:T(2,128)S(1)}, u32[]{:S(2)}) copy-start(f32[394,2]{0,1:T(2,128)S(1)} %select_reduce_fusion.1) | copy-start | bytes 9460
  106.7 26.5 %all-to-all-start.2 = ((bf16[4,248,768]{2,1,0:T(8,128)(2,1)}), bf16[4,248,768]{2,1,0:T(8,128)(2,1)}, u32[]{:S(2)}, u32[]{:S(2)}) async-start(bf16[4,248,768]{2,1,0:T(8,128)(2,1)} %bitcast.132), calls=%async_computation.2 | async-start | bytes 3047424 | tf_op jit(solution)/shard_map/all_to_all | solution.py:115
  118.3 4.5 copy-start.59
  149.8 40.4 %all-to-all-start.1 = ((bf16[4,248,768]{2,1,0:T(8,128)(2,1)}), bf16[4,248,768]{2,1,0:T(8,128)(2,1)}, u32[]{:S(2)}, u32[]{:S(2)}) async-start(bf16[4,248,768]{2,1,0:T(8,128)(2,1)} %bitcast.130), calls=%async_computation.1 | async-start | bytes 3047424 | tf_op jit(solution)/shard_map/all_to_all | solution.py:95
  154.2 85.3 %reduce-scatter.10.cloned.1.call-start = ((), (), s32[]{:S(2)}) async-start(), calls=%async_computation.9 | async-start | bytes 1474560 | tf_op jit(solution)/shard_map/reduce_scatter | solution.py:230
  164.6 7.8 %collective-permute-start = (bf16[1,248,768]{2,1,0:T(8,128)(2,1)}, bf16[1,248,768]{2,1,0:T(8,128)(2,1)}, u32[]{:S(2)}, u32[]{:S(2)}) collective-permute-start(bf16[1,248,768]{2,1,0:T(8,128)(2,1)} %get-tuple-element.92), channel_id=1, source_target_pairs={{0,1},{1,0},{2,3},{3,2},{4,5},{5,4},{6,7},{7,6},{8,9},{9,8},{10,11... | collective-permute-start | bytes 1142792 | tf_op jit(solution)/shard_map/ppermute | solution.py:146
  165.1 17.4 %collective-permute-start.1 = (bf16[1,248,768]{2,1,0:T(8,128)(2,1)}, bf16[1,248,768]{2,1,0:T(8,128)(2,1)}, u32[]{:S(2)}, u32[]{:S(2)}) collective-permute-start(bf16[1,248,768]{2,1,0:T(8,128)(2,1)} %get-tuple-element.91), channel_id=1, source_target_pairs={{0,2},{1,3},{2,0},{3,1},{4,6},{5,7},{6,4},{7,5},{8,10},{9,11},{10,... | collective-permute-start | bytes 1142792 | tf_op jit(solution)/shard_map/ppermute | solution.py:146
  168.9 21.3 %copy-start.41 = (s32[2,394]{1,0:T(2,128)S(1)}, s32[2,394]{1,0:T(2,128)}, u32[]{:S(2)}) copy-start(s32[2,394]{1,0:T(2,128)} %copy-done.39) | copy-start | bytes 9460
  168.9 21.3 %copy-start.54 = (f32[394,2]{0,1:T(2,128)S(1)}, f32[394,2]{0,1:T(2,128)}, u32[]{:S(2)}) copy-start(f32[394,2]{0,1:T(2,128)} %copy-done.53) | copy-start | bytes 9460
  171.0 18.5 %collective-permute-start.2 = (bf16[1,248,768]{2,1,0:T(8,128)(2,1)}, bf16[1,248,768]{2,1,0:T(8,128)(2,1)S(1)}, u32[]{:S(2)}, u32[]{:S(2)}) collective-permute-start(bf16[1,248,768]{2,1,0:T(8,128)(2,1)} %get-tuple-element.90), channel_id=1, source_target_pairs={{0,3},{1,2},{2,1},{3,0},{4,7},{5,6},{6,5},{7,4},{8,11},{9,10},{10,... | collective-permute-start | bytes 1142792 | tf_op jit(solution)/shard_map/ppermute | solution.py:146
  190.2 4.4 copy-start.3
  190.3 4.4 copy-start.17
  190.3 4.4 copy-start.21
  190.3 4.4 copy-start.34
  190.3 4.4 copy-start.36
  207.3 70.3 %reduce-scatter.8.cloned.1.call-start = ((), (), s32[]{:S(2)}) async-start(), calls=%async_computation.8 | async-start | bytes 4423680 | tf_op jit(solution)/shard_map/reduce_scatter | solution.py:227
  207.5 10.3 %slice-start = ((s8[4915200]{0:T(1024)(128)(4,1)}), s8[4194304]{0:T(1024)(128)(4,1)S(1)}, s32[]{:S(2)}) async-start(s8[4915200]{0:T(1024)(128)(4,1)} %bitcast.128), calls=%async_computation.14 | async-start | bytes 8388608
  212.0 5.9 slice-start.1
  235.9 96.5 %reduce-scatter.16.cloned.1.call-start = ((), (), s32[]{:S(2)}) async-start(), calls=%async_computation.12 | async-start | bytes 245760
  239.4 144.8 %all-reduce.10.cloned.1.call-start = ((), (), s32[]{:S(2)}) async-start(), calls=%async_computation.13 | async-start | bytes 2359296 | tf_op jit(solution)/shard_map/psum | solution.py:250
  277.6 204.9 %reduce-scatter.12.cloned.1.call-start = ((), (), s32[]{:S(2)}) async-start(), calls=%async_computation.10 | async-start | bytes 5308416 | tf_op jit(solution)/shard_map/reduce_scatter | solution.py:149
  287.1 294.3 %reduce-scatter.14.cloned.1.call-start = ((), (), s32[]{:S(2)}) async-start(), calls=%async_computation.11 | async-start | bytes 5308416 | tf_op jit(solution)/shard_map/reduce_scatter | solution.py:124
  327.9 5.3 copy-start.56
  327.9 5.3 copy-start.57
  (42 other events, 93.7 us)
Sparse Core Ops, SparseCore 0:
  207.4 26.8 reduce-scatter.9
  236.8 40.7 reduce-scatter.7
  280.6 19.7 reduce-scatter.15
  303.8 80.2 all-reduce.9
  387.7 94.7 reduce-scatter.11
  486.0 95.3 reduce-scatter.13
